TPU v7x, 32 devices: a 4x4x1 block of a 4x4x8 slice. The times are simulated.
32 devices in a mesh: rep: 1 (over z), dp: 32 (over y, x, core).
Axes of the slice: x: 4, y: 4, z: 1, core: 2. Of those that a mesh axis runs over, the one named last changes fastest.
The devices are a block of a 4x4x8 slice.
Arguments:
- tokens: int32 [2, 96], P(None, ('rep', 'dp'))
- start_pos: int32 [96], P(('rep', 'dp'))
- k_cache: bfloat16 [2, 96, 12, 1024, 64], P(None, ('rep', 'dp'))
- v_cache: bfloat16 [2, 96, 12, 1024, 64], P(None, ('rep', 'dp'))
- tok_table: bfloat16 [50272, 768], P('dp')
- pos_table: bfloat16 [2048, 768], P('dp')
- ln1_gain: bfloat16 [2, 768], P(None, 'dp')
- ln1_bias: bfloat16 [2, 768], P(None, 'dp')
- w_q: bfloat16 [2, 768, 768], P(None, 'dp')
- w_k: bfloat16 [2, 768, 768], P(None, 'dp')
- w_v: bfloat16 [2, 768, 768], P(None, 'dp')
- b_q: bfloat16 [2, 768], P(None, 'dp')
- b_k: bfloat16 [2, 768], P(None, 'dp')
- b_v: bfloat16 [2, 768], P(None, 'dp')
- w_o: bfloat16 [2, 768, 768], P(None, 'dp')
- b_o: bfloat16 [2, 768], P(None, 'dp')
- ln2_gain: bfloat16 [2, 768], P(None, 'dp')
- ln2_bias: bfloat16 [2, 768], P(None, 'dp')
- w_fc1: bfloat16 [2, 768, 3072], P(None, 'dp')
- b_fc1: bfloat16 [2, 3072], P(None, 'dp')
- w_fc2: bfloat16 [2, 3072, 768], P(None, 'dp')
- b_fc2: bfloat16 [2, 768], P(None, 'dp')
- lnf_gain: bfloat16 [768], P('dp')
- lnf_bias: bfloat16 [768], P('dp')
Outputs:
- output 1: float32 [2, 96, 50272], P(None, ('rep', 'dp'))
- output 2: bfloat16 [2, 96, 12, 1024, 64], P(None, ('rep', 'dp'))
- output 3: bfloat16 [2, 96, 12, 1024, 64], P(None, ('rep', 'dp'))
All inputs are finite; a program needn't handle non-finite values.
Results may differ from a plain program's by a relative error of at most 0.00434985.
Values are sent between devices in bfloat16 or wider.
A program may use at most 768 MiB of HBM per device.

v0:
```python
import jax
import jax.numpy as jnp
from jax import lax
from jax.sharding import PartitionSpec as P

EPS = 1e-5


def layer_norm(resid_in, gain, shift):
    mean = jnp.mean(resid_in, axis=-1, keepdims=True)
    variance = jnp.mean(jnp.square(resid_in - mean), axis=-1, keepdims=True)
    normed = (resid_in - mean) * lax.rsqrt(variance + EPS)
    return (normed * gain.astype(jnp.float32) + shift.astype(jnp.float32)).astype(jnp.bfloat16)


def write_slot(cache_layer, fresh, cur_pos):
    slots = jnp.arange(cache_layer.shape[2], dtype=jnp.int32)
    hit_mask = (slots[None, :] == cur_pos[:, None])[:, None, :, None]
    return jnp.where(hit_mask, fresh[:, :, None, :], cache_layer)


def attend(query, k_layer, v_layer, cur_pos):
    scores = jnp.einsum('bhd,bhsd->bhs', query, k_layer, preferred_element_type=jnp.float32)
    slots = jnp.arange(k_layer.shape[2], dtype=jnp.int32)
    valid = (slots[None, :] <= cur_pos[:, None])[:, None, :]
    scores = jnp.where(valid, scores, -1e30)
    attn_probs = jax.nn.softmax(scores, axis=-1).astype(jnp.bfloat16)
    return jnp.einsum('bhs,bhsd->bhd', attn_probs, v_layer, preferred_element_type=jnp.float32).astype(jnp.bfloat16)


def layer_step(residual, cur_pos, k_layer, v_layer, params):
    ln1_g, ln1_b, w_q, w_k, w_v, b_q, b_k, b_v, w_o, b_o, ln2_g, ln2_b, w_fc1, b_fc1, w_fc2, b_fc2 = params
    rows = k_layer.shape[0]
    heads = k_layer.shape[1]
    head_dim = k_layer.shape[3]
    hidden = layer_norm(residual, ln1_g, ln1_b)
    query = ((jnp.dot(hidden, w_q, preferred_element_type=jnp.float32) + b_q.astype(jnp.float32)) * head_dim ** -0.5).astype(jnp.bfloat16)
    k_fresh = (jnp.dot(hidden, w_k, preferred_element_type=jnp.float32) + b_k.astype(jnp.float32)).astype(jnp.bfloat16)
    v_fresh = (jnp.dot(hidden, w_v, preferred_element_type=jnp.float32) + b_v.astype(jnp.float32)).astype(jnp.bfloat16)
    k_layer = write_slot(k_layer, k_fresh.reshape(rows, heads, head_dim), cur_pos)
    v_layer = write_slot(v_layer, v_fresh.reshape(rows, heads, head_dim), cur_pos)
    attn_out = attend(query.reshape(rows, heads, head_dim), k_layer, v_layer, cur_pos)
    residual = residual + jnp.dot(attn_out.reshape(rows, heads * head_dim), w_o, preferred_element_type=jnp.float32) + b_o.astype(jnp.float32)
    hidden = layer_norm(residual, ln2_g, ln2_b)
    hidden_act = jax.nn.relu(jnp.dot(hidden, w_fc1, preferred_element_type=jnp.float32) + b_fc1.astype(jnp.float32)).astype(jnp.bfloat16)
    residual = residual + jnp.dot(hidden_act, w_fc2, preferred_element_type=jnp.float32) + b_fc2.astype(jnp.float32)
    return residual, k_layer, v_layer


def solution(mesh):
    batch_axes = ('rep', 'dp')
    mat_spec = P(None, 'dp', None)
    vec_spec = P(None, 'dp')
    in_specs = (P(None, batch_axes), P(batch_axes), P(None, batch_axes), P(None, batch_axes), P('dp', None), P('dp', None), vec_spec, vec_spec, mat_spec, mat_spec, mat_spec, vec_spec, vec_spec, vec_spec, mat_spec, vec_spec, vec_spec, vec_spec, mat_spec, vec_spec, mat_spec, vec_spec, P('dp'), P('dp'))
    out_specs = (P(None, batch_axes, None), P(None, batch_axes), P(None, batch_axes))

    def gather(piece):
        return lax.all_gather(piece, 'dp', axis=0, tiled=True)

    def body(tokens, start_pos, k_cache, v_cache, tok_table, pos_table, ln1_gain, ln1_bias, w_q, w_k, w_v, b_q, b_k, b_v, w_o, b_o, ln2_gain, ln2_bias, w_fc1, b_fc1, w_fc2, b_fc2, lnf_gain, lnf_bias):
        stacked = (ln1_gain, ln1_bias, w_q, w_k, w_v, b_q, b_k, b_v, w_o, b_o, ln2_gain, ln2_bias, w_fc1, b_fc1, w_fc2, b_fc2)
        layers = k_cache.shape[0]
        k_layers = [k_cache[layer] for layer in range(layers)]
        v_layers = [v_cache[layer] for layer in range(layers)]
        outputs = []
        for step in range(tokens.shape[0]):
            table = gather(tok_table)
            positions = gather(pos_table)
            cur_pos = start_pos + step
            residual = jnp.take(table, tokens[step], axis=0).astype(jnp.float32) + jnp.take(positions, cur_pos, axis=0).astype(jnp.float32)
            for layer in range(layers):
                params = tuple(gather(piece[layer]) for piece in stacked)
                residual, k_layers[layer], v_layers[layer] = layer_step(residual, cur_pos, k_layers[layer], v_layers[layer], params)
            final = layer_norm(residual, gather(lnf_gain), gather(lnf_bias))
            outputs.append(jnp.einsum('bd,vd->bv', final, table, preferred_element_type=jnp.float32))
        return jnp.stack(outputs), jnp.stack(k_layers), jnp.stack(v_layers)

    return jax.shard_map(body, mesh=mesh, in_specs=in_specs, out_specs=out_specs, check_vma=False)
```

profile of v0, /device:TPU:97, one launch (start us, length us, event | category | flops | bytes accessed | tf_op | source)
XLA Modules:
  0.0 868.4 jit_solution(11168121972449521054)
XLA Ops:
  28.2 51.8 %all-reduce.22 = (bf16[768]{0:T(1024)(128)(2,1)S(1)}, bf16[768]{0:T(1024)(128)(2,1)S(1)}, bf16[768]{0:T(1024)(128)(2,1)S(1)}, bf16[768]{0:T(1024)(128)(2,1)S(1)}...) all-reduce(bf16[768]{0:T(1024)(128)(2,1)S(1)} %dynamic-update-slice, ...), channel_id=9, replica_groups=mesh['rep'=1,'dp'=32] {'dp'}, use_global_device_ids=true, to_apply=%add.4 | all-reduce | flops 21504 | bytes 86016
  80.5 2.9 gather_fusion.3
  83.3 2.9 gather_fusion.1
  86.2 193.0 %all-gather.74.cloned.1.call-done = bf16[32,1571,768]{2,1,0:T(8,128)(2,1)} async-done(((bf16[1,1571,768]{2,1,0:T(8,128)(2,1)}), bf16[32,1571,768]{2,1,0:T(8,128)(2,1)}) %all-gather.74.cloned.1.call-update) | async-done | bytes 77217808 | tf_op jit(solution)/shard_map/all_gather | solution.py:58
  279.2 74.7 %reshape.409 = bf16[50272,768]{1,0:T(8,128)(2,1)} reshape(bf16[32,1571,768]{2,1,0:T(8,128)(2,1)} %all-gather.74.cloned.1.call-done) | data formatting | bytes 154435584
  362.5 33.2 %all-gather.52.cloned.1.call-done = bf16[1,768,768]{2,1,0:T(8,128)(2,1)} async-done(((bf16[1,24,768]{2,1,0:T(8,128)(2,1)}), bf16[1,768,768]{2,1,0:T(8,128)(2,1)}) %all-gather.52.cloned.1.call-update) | async-done | bytes 1179664 | tf_op jit(solution)/shard_map/all_gather | solution.py:58
  399.0 3.2 fusion.30
  402.5 3.9 fusion.28
  406.9 3.1 fusion.36
  410.2 3.8 fusion.37
  414.0 20.7 %all-gather.56.cloned.1.call-done = bf16[1,768,768]{2,1,0:T(8,128)(2,1)} async-done(((bf16[1,24,768]{2,1,0:T(8,128)(2,1)}), bf16[1,768,768]{2,1,0:T(8,128)(2,1)}) %all-gather.56.cloned.1.call-update) | async-done | bytes 1179664 | tf_op jit(solution)/shard_map/all_gather | solution.py:58
  438.5 39.7 %all-gather.60.cloned.1.call-done = bf16[1,3072,768]{2,1,0:T(8,128)(2,1)} async-done(((bf16[1,96,768]{2,1,0:T(8,128)(2,1)}), bf16[1,3072,768]{2,1,0:T(8,128)(2,1)}) %all-gather.60.cloned.1.call-update) | async-done | bytes 4718608 | tf_op jit(solution)/shard_map/all_gather | solution.py:58
  478.3 43.0 %all-gather.58.cloned.1.call-done = bf16[1,768,3072]{2,1,0:T(8,128)(2,1)} async-done(((bf16[1,24,3072]{2,1,0:T(8,128)(2,1)}), bf16[1,768,3072]{2,1,0:T(8,128)(2,1)}) %all-gather.58.cloned.1.call-update) | async-done | bytes 4718608 | tf_op jit(solution)/shard_map/all_gather | solution.py:58
  521.3 5.4 fusion.362
  526.9 5.4 fusion.365
  532.6 27.8 %all-gather.66.cloned.1.call-done = bf16[1,768,768]{2,1,0:T(8,128)(2,1)} async-done(((bf16[1,24,768]{2,1,0:T(8,128)(2,1)}), bf16[1,768,768]{2,1,0:T(8,128)(2,1)}) %all-gather.66.cloned.1.call-update) | async-done | bytes 1179664 | tf_op jit(solution)/shard_map/all_gather | solution.py:58
  563.6 35.6 %all-gather.62.cloned.1.call-done = bf16[1,768,768]{2,1,0:T(8,128)(2,1)} async-done(((bf16[1,24,768]{2,1,0:T(8,128)(2,1)}), bf16[1,768,768]{2,1,0:T(8,128)(2,1)}) %all-gather.62.cloned.1.call-update) | async-done | bytes 1179664 | tf_op jit(solution)/shard_map/all_gather | solution.py:58
  600.8 37.4 %all-gather.64.cloned.1.call-done = bf16[1,768,768]{2,1,0:T(8,128)(2,1)} async-done(((bf16[1,24,768]{2,1,0:T(8,128)(2,1)}), bf16[1,768,768]{2,1,0:T(8,128)(2,1)}) %all-gather.64.cloned.1.call-update) | async-done | bytes 1179664 | tf_op jit(solution)/shard_map/all_gather | solution.py:58
  641.5 3.2 fusion.26
  644.9 3.8 fusion.24
  648.8 28.3 %all-gather.68.cloned.1.call-done = bf16[1,768,768]{2,1,0:T(8,128)(2,1)} async-done(((bf16[1,24,768]{2,1,0:T(8,128)(2,1)}), bf16[1,768,768]{2,1,0:T(8,128)(2,1)}) %all-gather.68.cloned.1.call-update) | async-done | bytes 1179664 | tf_op jit(solution)/shard_map/all_gather | solution.py:58
  679.2 13.2 %select_select_fusion.1 = (bf16[1,3,12,1024,64]{3,4,2,1,0:T(8,128)(2,1)}, bf16[1,3,12,1024,64]{3,4,2,1,0:T(8,128)(2,1)}, bf16[1,3,12,1024,64]{3,4,2,1,0:T(8,128)(2,1)}, bf16[1,3,12,1024,64]{3,4,2,1,0:T(8,128)(2,1)}) fusion(pred[3,1024]{1,0:T(4,128)(4,1)S(1)} %get-tuple-element.68, pred[3,1024]{1,0:T(4,128)(4,1)S(1)} %get-tuple-element.70, ...), kind=kLoop, calls=%fused_computation.37 | loop fusion | flops 18874368 | bytes 37791744 | tf_op jit(solution)/shard_map/jit(_where)/select_n | solution.py:19
  692.4 28.3 %all-gather.72.cloned.1.call-done = bf16[1,3072,768]{2,1,0:T(8,128)(2,1)} async-done(((bf16[1,96,768]{2,1,0:T(8,128)(2,1)}), bf16[1,3072,768]{2,1,0:T(8,128)(2,1)}) %all-gather.72.cloned.1.call-update) | async-done | bytes 4718608 | tf_op jit(solution)/shard_map/all_gather | solution.py:58
  720.7 43.4 %all-gather.70.cloned.1.call-done = bf16[1,768,3072]{2,1,0:T(8,128)(2,1)} async-done(((bf16[1,24,3072]{2,1,0:T(8,128)(2,1)}), bf16[1,768,3072]{2,1,0:T(8,128)(2,1)}) %all-gather.70.cloned.1.call-update) | async-done | bytes 4718608 | tf_op jit(solution)/shard_map/all_gather | solution.py:58
  764.1 5.4 fusion.369
  770.1 3.1 fusion.38
  773.5 3.8 fusion.39
  778.0 5.4 fusion.373
  783.6 29.3 %convolution_bitcast_fusion = f32[1,3,50272]{2,1,0:T(4,128)S(1)} fusion(bf16[50272,768]{1,0:T(8,128)(2,1)} %reshape.409, f32[3,768]{1,0:T(4,128)S(1)} %get-tuple-element.105, f32[3]{0:T(128)S(1)} %add_rsqrt_fusion, f32[3]{0:T(128)S(1)} %broadcast_multiply_fusion, f32[768]{0:T(1024)S(1)} %convert_element_type.241, f32[768]{0:T(1024)S(1)} %convert_element_type.240), kind=kOutput, calls=%fused_computation.12 | convolution fusion | flops 231664896 | bytes 77836440 | tf_op jit(solution)/shard_map/bd,vd->bv/dot_general | solution.py:75
  812.9 29.6 %convolution_bitcast_fusion.1 = f32[1,3,50272]{2,1,0:T(4,128)S(1)} fusion(bf16[50272,768]{1,0:T(8,128)(2,1)} %reshape.409, f32[3,768]{1,0:T(4,128)S(1)} %get-tuple-element.109, f32[768]{0:T(1024)S(1)} %convert_element_type.241, f32[768]{0:T(1024)S(1)} %convert_element_type.240, f32[3]{0:T(128)S(1)} %add_rsqrt_fusion.5, f32[3]{0:T(128)S(1)} %broadcast_multiply_fusion.5), kind=kOutput, calls=%fused_computation.13 | convolution fusion | flops 231664896 | bytes 77836440 | tf_op jit(solution)/shard_map/bd,vd->bv/dot_general | solution.py:75
  844.6 8.4 pad_maximum_fusion
  852.9 8.4 pad_maximum_fusion.1
  (232 shorter events, 52.2 us)
Async XLA Ops:
  7.2 16.0 %copy-start.2 = (s32[3]{0:T(128)S(1)}, s32[3]{0:T(128)}, u32[]{:S(2)}) copy-start(s32[3]{0:T(128)} %param.29) | copy-start | bytes 40
  7.2 16.1 %copy-start.3 = (bf16[2,24]{1,0:T(2,128)(2,1)S(1)}, bf16[2,24]{1,0:T(2,128)(2,1)}, u32[]{:S(2)}) copy-start(bf16[2,24]{1,0:T(2,128)(2,1)} %param.41) | copy-start | bytes 292
  7.2 16.2 %copy-start.4 = (bf16[2,24]{1,0:T(2,128)(2,1)S(1)}, bf16[2,24]{1,0:T(2,128)(2,1)}, u32[]{:S(2)}) copy-start(bf16[2,24]{1,0:T(2,128)(2,1)} %param.35) | copy-start | bytes 292
  7.2 16.2 %copy-start.5 = (bf16[2,24]{1,0:T(2,128)(2,1)S(1)}, bf16[2,24]{1,0:T(2,128)(2,1)}, u32[]{:S(2)}) copy-start(bf16[2,24]{1,0:T(2,128)(2,1)} %param.34) | copy-start | bytes 292
  7.2 16.2 %copy-start.6 = (bf16[2,24]{1,0:T(2,128)(2,1)S(1)}, bf16[2,24]{1,0:T(2,128)(2,1)}, u32[]{:S(2)}) copy-start(bf16[2,24]{1,0:T(2,128)(2,1)} %param.39) | copy-start | bytes 292
  7.2 16.2 %copy-start.7 = (bf16[2,24]{1,0:T(2,128)(2,1)S(1)}, bf16[2,24]{1,0:T(2,128)(2,1)}, u32[]{:S(2)}) copy-start(bf16[2,24]{1,0:T(2,128)(2,1)} %param.40) | copy-start | bytes 292
  7.2 16.2 %copy-start.8 = (bf16[2,24]{1,0:T(2,128)(2,1)S(1)}, bf16[2,24]{1,0:T(2,128)(2,1)}, u32[]{:S(2)}) copy-start(bf16[2,24]{1,0:T(2,128)(2,1)} %param.43) | copy-start | bytes 292
  7.3 16.2 %copy-start.9 = (bf16[2,96]{1,0:T(2,128)(2,1)S(1)}, bf16[2,96]{1,0:T(2,128)(2,1)}, u32[]{:S(2)}) copy-start(bf16[2,96]{1,0:T(2,128)(2,1)} %param.47) | copy-start | bytes 1156
  7.3 16.2 %copy-start.10 = (bf16[2,24]{1,0:T(2,128)(2,1)S(1)}, bf16[2,24]{1,0:T(2,128)(2,1)}, u32[]{:S(2)}) copy-start(bf16[2,24]{1,0:T(2,128)(2,1)} %param.49) | copy-start | bytes 292
  7.3 16.3 %copy-start.11 = (bf16[2,24]{1,0:T(2,128)(2,1)S(1)}, bf16[2,24]{1,0:T(2,128)(2,1)}, u32[]{:S(2)}) copy-start(bf16[2,24]{1,0:T(2,128)(2,1)} %param.45) | copy-start | bytes 292
  7.3 16.3 %copy-start.12 = (bf16[2,24]{1,0:T(2,128)(2,1)S(1)}, bf16[2,24]{1,0:T(2,128)(2,1)}, u32[]{:S(2)}) copy-start(bf16[2,24]{1,0:T(2,128)(2,1)} %param.44) | copy-start | bytes 292
  7.3 20.5 %copy-start.15 = (bf16[24]{0:T(256)(128)(2,1)S(1)}, bf16[24]{0:T(256)(128)(2,1)}, u32[]{:S(2)}) copy-start(bf16[24]{0:T(256)(128)(2,1)} %param.51) | copy-start | bytes 148
  7.3 20.7 %copy-start.16 = (bf16[24]{0:T(256)(128)(2,1)S(1)}, bf16[24]{0:T(256)(128)(2,1)}, u32[]{:S(2)}) copy-start(bf16[24]{0:T(256)(128)(2,1)} %param.50) | copy-start | bytes 148
  7.3 72.9 %copy-start.13 = (s32[2,3]{1,0:T(2,128)S(1)}, s32[2,3]{1,0:T(2,128)}, u32[]{:S(2)}) copy-start(s32[2,3]{1,0:T(2,128)} %param.28) | copy-start | bytes 76
  7.3 73.1 %all-gather.48.cloned.1.call-start = ((), (), s32[]{:S(2)}) async-start(), calls=%async_computation | async-start | bytes 3244032 | tf_op jit(solution)/shard_map/all_gather | solution.py:58
  8.1 271.1 %all-gather.74.cloned.1.call-start = ((), (), s32[]{:S(2)}) async-start(), calls=%async_computation.13 | async-start | bytes 79884288 | tf_op jit(solution)/shard_map/all_gather | solution.py:58
  8.9 348.5 %all-gather.54.cloned.1.call-start = ((), (), s32[]{:S(2)}) async-start(), calls=%async_computation.3 | async-start | bytes 1216512 | tf_op jit(solution)/shard_map/all_gather | solution.py:58
  10.5 350.3 %all-gather.50.cloned.1.call-start = ((), (), s32[]{:S(2)}) async-start(), calls=%async_computation.1 | async-start | bytes 1216512 | tf_op jit(solution)/shard_map/all_gather | solution.py:58
  12.0 383.6 %all-gather.52.cloned.1.call-start = ((), (), s32[]{:S(2)}) async-start(), calls=%async_computation.2 | async-start | bytes 1216512 | tf_op jit(solution)/shard_map/all_gather | solution.py:58
  13.6 421.1 %all-gather.56.cloned.1.call-start = ((), (), s32[]{:S(2)}) async-start(), calls=%async_computation.4 | async-start | bytes 1216512 | tf_op jit(solution)/shard_map/all_gather | solution.py:58
  15.2 463.1 %all-gather.60.cloned.1.call-start = ((), (), s32[]{:S(2)}) async-start(), calls=%async_computation.6 | async-start | bytes 4866048 | tf_op jit(solution)/shard_map/all_gather | solution.py:58
  17.0 504.3 %all-gather.58.cloned.1.call-start = ((), (), s32[]{:S(2)}) async-start(), calls=%async_computation.5 | async-start | bytes 4866048 | tf_op jit(solution)/shard_map/all_gather | solution.py:58
  18.9 541.5 %all-gather.66.cloned.1.call-start = ((), (), s32[]{:S(2)}) async-start(), calls=%async_computation.9 | async-start | bytes 1216512 | tf_op jit(solution)/shard_map/all_gather | solution.py:58
  19.7 579.5 %all-gather.62.cloned.1.call-start = ((), (), s32[]{:S(2)}) async-start(), calls=%async_computation.7 | async-start | bytes 1216512 | tf_op jit(solution)/shard_map/all_gather | solution.py:58
  20.3 617.9 %all-gather.64.cloned.1.call-start = ((), (), s32[]{:S(2)}) async-start(), calls=%async_computation.8 | async-start | bytes 1216512 | tf_op jit(solution)/shard_map/all_gather | solution.py:58
  21.1 656.0 %all-gather.68.cloned.1.call-start = ((), (), s32[]{:S(2)}) async-start(), calls=%async_computation.10 | async-start | bytes 1216512 | tf_op jit(solution)/shard_map/all_gather | solution.py:58
  21.8 698.9 %all-gather.72.cloned.1.call-start = ((), (), s32[]{:S(2)}) async-start(), calls=%async_computation.12 | async-start | bytes 4866048 | tf_op jit(solution)/shard_map/all_gather | solution.py:58
  22.6 741.6 %all-gather.70.cloned.1.call-start = ((), (), s32[]{:S(2)}) async-start(), calls=%async_computation.11 | async-start | bytes 4866048 | tf_op jit(solution)/shard_map/all_gather | solution.py:58
  402.5 4.0 copy-start.14
  692.4 77.3 %copy-start = (bf16[1,768,768]{2,1,0:T(8,128)(2,1)S(1)}, bf16[1,768,768]{2,1,0:T(8,128)(2,1)}, u32[]{:S(2)}) copy-start(bf16[1,768,768]{2,1,0:T(8,128)(2,1)} %all-gather.62.cloned.1.call-done) | copy-start | bytes 3538948
  773.5 4.0 copy-start.1
Sparse Core Ops, SparseCore 0:
  10.2 44.4 all-gather.47
  56.9 222.3 all-gather.73
  281.4 36.4 all-gather.53
  319.9 36.8 all-gather.49
  358.7 36.8 all-gather.51
  397.7 36.9 all-gather.55
  437.3 40.8 all-gather.59
  480.3 40.9 all-gather.57
  523.4 36.8 all-gather.65
  562.4 36.8 all-gather.61
  601.4 36.8 all-gather.63
  640.2 36.8 all-gather.67
  679.7 40.8 all-gather.71
  723.2 40.9 all-gather.69
where the time goes:
time: 876 us; the launch traced here: 868 us
  waiting for transfers between devices  536 us (61%)
  matrix products  130 us (15%)
  local copies, waits for them, and re-layouts  100 us (11%)
  blocking collectives  51.8 us (6%)
  other arithmetic  33.7 us (4%)
  between operations  15.3 us (2%)
    all_gather x14, waiting for transfers between devices, gather(): return lax.all_gather(piece, 'dp', axis=0, tiled=True)  531 us
    unnamed x90, local copies, waits for them, and re-layouts  81.1 us
    dot_general x2, matrix products, body(): jnp.einsum('bd,vd->bv', final, table, preferred_element_type=jnp.float32)  58.9 us
    unnamed x1, blocking collectives  51.8 us
    dot_general x4, matrix products, layer_step(): jnp.dot(hidden_act, w_fc2, preferred_element_type=jnp.float32)  21.5 us
  transfers between devices with their start and end apart: 14, of which 11 were waited for; matrix products, arithmetic and copies ran while one was open for 19% of the time, Pallas kernels for 0%

commit v1 on v0

v1 whole, which is shorter than its diff:
```python
import functools
import math

import jax
import jax.numpy as jnp
from jax import lax
from jax.experimental import pallas as pl
from jax.experimental.pallas import tpu as pltpu
from jax.sharding import PartitionSpec as P

EPS = 1e-5
LANES = 128
SLOT = 8
MESH = pl.DeviceIdType.MESH
F32 = jnp.float32
BF16 = jnp.bfloat16
NT = (((1,), (1,)), ((), ()))


def dot(a, b):
    return jnp.dot(a, b, preferred_element_type=F32)


def dot_nt(a, b):
    return lax.dot_general(a, b, NT, preferred_element_type=F32)


def iota(shape, dim):
    return lax.broadcasted_iota(jnp.int32, shape, dim)


def layer_norm(x, gain, shift):
    mean = jnp.mean(x, axis=-1, keepdims=True)
    variance = jnp.mean(jnp.square(x - mean), axis=-1, keepdims=True)
    return ((x - mean) * lax.rsqrt(variance + EPS) * gain + shift).astype(BF16)


def decode_kernel(n, dims, pos_ref, tp_ref, tok_hbm, tok_tail, pos_tab, wa_ref, fs_ref, w2_ref, b1_ref, kc_hbm, vc_hbm,
                  lrecv, kv_out,
                  t_buf, e_buf, c_send, r_buf, w_buf, f_buf, k_buf, v_buf, h_src, h_buf, p_send, p_recv, l_send,
                  loc_sem, s_sem, r_sem, sw_sem, w1_sem, w2_sem, wd_sem):
    layers, seqs, heads, steps = dims
    me = lax.axis_index("dp")
    side = math.isqrt(n // 2)
    core = lax.rem(me, 2)
    cx = lax.rem(me // 2, side)
    cy = me // (2 * side)
    d = pos_tab.shape[1]
    head_dim = d // heads
    share = wa_ref.shape[1]
    wcols = wa_ref.shape[2]
    half = wcols // 2
    vocab_rows = tok_hbm.shape[0]
    main = e_buf.shape[0] - LANES
    ff = w2_ref.shape[0]
    ff_share = b1_ref.shape[1] // layers

    def dev(y, x, c):
        return (y * side + x) * 2 + c

    def remote(src, dst, ssem, rsem, peer):
        return pltpu.make_async_remote_copy(src_ref=src, dst_ref=dst, send_sem=ssem, recv_sem=rsem,
                                            device_id={"dp": peer}, device_id_type=MESH)

    def rows(ref, j, size):
        return ref.at[pl.ds(pl.multiple_of(j * size, SLOT), size)]

    e_copy = pltpu.make_async_copy(tok_hbm.at[pl.ds(0, main)], e_buf.at[pl.ds(0, main)], loc_sem.at[0])
    e_copy.start()
    cache_copies = []
    for l in range(layers):
        pair = (pltpu.make_async_copy(kc_hbm.at[l], k_buf.at[l], loc_sem.at[1 + 2 * l]),
                pltpu.make_async_copy(vc_hbm.at[l], v_buf.at[l], loc_sem.at[2 + 2 * l]))
        for copy in pair:
            copy.start()
        cache_copies.append(pair)

    barrier = pltpu.get_barrier_semaphore()

    def greet(r, carry):
        pl.semaphore_signal(barrier, inc=1, device_id={"dp": lax.rem(me + r, n)}, device_id_type=MESH)
        return carry

    lax.fori_loop(1, n, greet, 0)
    pl.semaphore_wait(barrier, n - 1)

    def broadcast(src, buf, size, k):
        def one(r, carry):
            remote(src, rows(buf, me, size), s_sem.at[k], r_sem.at[k], lax.rem(me + r, n)).start()
            return carry
        lax.fori_loop(1, n, one, 0)

    def scatter(src, buf, size, k):
        def one(r, carry):
            peer = lax.rem(me + r, n)
            remote(rows(src, peer, size), rows(buf, me, size), s_sem.at[k], r_sem.at[k], peer).start()
            return carry
        lax.fori_loop(1, n, one, 0)

    def most(buf, size):
        return buf.at[pl.ds(0, (n - 1) * size)]

    def arrived(buf, size, k):
        remote(most(buf, size), most(buf, size), s_sem.at[k], r_sem.at[k], me).wait_recv()

    def sent(buf, size, k):
        remote(most(buf, size), most(buf, size), s_sem.at[k], r_sem.at[k], me).wait_send()

    def own(buf, size):
        return pl.ds(pl.multiple_of(me * size, SLOT), size)

    def block_dev(color, along, across):
        if color == 0:
            return dev(lax.rem(cy + side - across, side), lax.rem(cx + side - along, side), core)
        return dev(lax.rem(cy + side - along, side), lax.rem(cx + side - across, side), core)

    def ring_peer(color, ring, step):
        if (color == 0) == (ring == 0):
            return dev(cy, lax.rem(cx + step, side), core)
        return dev(lax.rem(cy + step, side), cx, core)

    def wcol(color):
        return pl.ds(color * half, half)

    def wslot(l, color, j):
        return w_buf.at[l, pl.ds(pl.multiple_of(j * share, SLOT), share), wcol(color)]

    partner = dev(cy, cx, 1 - core)

    def gather_first(l):
        for color in range(2):
            for step in range(1, side):
                remote(wa_ref.at[l, :, wcol(color)], wslot(l, color, me), sw_sem.at[l, color],
                       w1_sem.at[l, color, step - 1], ring_peer(color, 0, step)).start()

    def gather_second(l):
        for along in range(side):
            for color in range(2):
                j = block_dev(color, along, 0)
                if along == 0:
                    src = wa_ref.at[l, :, wcol(color)]
                else:
                    src = wslot(l, color, j)
                    remote(src, src, sw_sem.at[l, color], w1_sem.at[l, color, along - 1], me).wait_recv()
                for step in range(1, side):
                    remote(src, wslot(l, color, j), sw_sem.at[l, color], w2_sem.at[l, color, along, step - 1],
                           ring_peer(color, 1, step)).start()
                remote(src, wslot(l, color, j), sw_sem.at[l, color], wd_sem.at[l], partner).start()

    def gather_third(l):
        w_buf[l, own(w_buf, share), :] = wa_ref[l]
        for across in range(1, side):
            for along in range(side):
                for color in range(2):
                    src = wslot(l, color, block_dev(color, along, across))
                    remote(src, src, sw_sem.at[l, color], w2_sem.at[l, color, along, across - 1], me).wait_recv()
                    remote(src, src, sw_sem.at[l, color], wd_sem.at[l], partner).start()

    def gather_wait(l):
        part = w_buf.at[l, pl.ds(0, n // 2 * share)]
        remote(part, part, sw_sem.at[l, 0], wd_sem.at[l], me).wait_recv()

    def gather_sent(l):
        for color in range(2):
            part = w_buf.at[l, pl.ds(0, (n - 1) * share), wcol(color)]
            remote(part, part, sw_sem.at[l, color], wd_sem.at[l], me).wait_send()

    TP, FC, EM, H0, P0 = 0, 1, 2, 3, 3 + layers + 1
    LG = P0 + layers

    broadcast(tp_ref, t_buf, SLOT, TP)
    t_buf[own(t_buf, SLOT), :] = tp_ref[...]
    gather_first(0)
    scatter(fs_ref, f_buf, share, FC)
    f_buf[own(f_buf, share), :] = fs_ref[own(fs_ref, share), :]
    e_buf[pl.ds(main, LANES), :] = tok_tail[...]
    e_copy.wait()
    arrived(t_buf, SLOT, TP)

    tokens = t_buf[:, 0:1] - me * vocab_rows
    places = t_buf[:, LANES // 2:LANES // 2 + 1] - me * pos_tab.shape[0]
    pick = (iota((n * SLOT, main + LANES), 1) == tokens).astype(F32).astype(BF16)
    c_send[:, 0:d] = dot(pick, e_buf[...]).astype(BF16)
    pick = (iota((n * SLOT, pos_tab.shape[0]), 1) == places).astype(F32).astype(BF16)
    c_send[:, d:2 * d] = dot(pick, pos_tab[...]).astype(BF16)
    scatter(c_send, r_buf, SLOT, EM)
    r_buf[own(r_buf, SLOT), :] = c_send[own(c_send, SLOT), :]

    gather_second(0)
    gather_first(1)

    arrived(f_buf, share, FC)
    vlane = layers * ff_share
    vcol = vlane // LANES * LANES
    count = 32
    select = (iota((count, LANES), 1) == iota((count, LANES), 0) + (vlane - vcol)).astype(F32).astype(BF16)
    vectors = dot_nt(select, f_buf[:, vcol:vcol + LANES])

    def vec(i, l):
        return vectors[layers * i + l:layers * i + l + 1, :]

    arrived(r_buf, SLOT, EM)
    found = jnp.sum(r_buf[...].astype(F32).reshape(n, SLOT, 2 * d), axis=0)
    x = found[:, 0:d] + found[:, d:2 * d]

    lane_head = iota((16, d), 1) // head_dim
    head_mask = lane_head == iota((16, d), 0)
    ff_lane = iota((n * SLOT, ff), 1)

    for l in range(layers):
        hidden = layer_norm(x, vec(0, l), vec(1, l))
        gather_third(l)
        gather_wait(l)
        q = ((dot(hidden, w_buf[l, :, 0:d]) + vec(2, l)) * head_dim ** -0.5).astype(BF16).astype(F32)
        k_new = (dot(hidden, w_buf[l, :, d:2 * d]) + vec(3, l)).astype(BF16)
        v_new = (dot(hidden, w_buf[l, :, 2 * d:3 * d]) + vec(4, l)).astype(BF16)
        kv_out[l, 0] = k_new
        kv_out[l, 1] = v_new
        v_wide = v_new.astype(F32)
        if l + 1 < layers:
            gather_second(l + 1)
        for copy in cache_copies[l]:
            copy.wait()
        outs = []
        for b in range(seqs):
            queries = jnp.concatenate(
                [jnp.where(head_mask, q[b * steps + t:b * steps + t + 1, :], 0.0) for t in range(steps)],
                axis=0).astype(BF16)
            scores = dot(queries, k_buf[l, b])
            scores = jnp.where(iota(scores.shape, 1) < pos_ref[b], scores, -1e30)
            fresh = dot_nt(queries, k_new)
            slot = iota(fresh.shape, 1) - b * steps
            fresh_ok = (slot >= 0) & (slot <= iota(fresh.shape, 0) // 16)
            fresh = jnp.where(fresh_ok, fresh, -1e30)
            top = jnp.maximum(jnp.max(scores, axis=-1, keepdims=True), jnp.max(fresh, axis=-1, keepdims=True))
            scores = jnp.exp(scores - top)
            fresh = jnp.exp(fresh - top)
            total = jnp.sum(scores, axis=-1, keepdims=True) + jnp.sum(fresh, axis=-1, keepdims=True)
            probs = (scores / total).astype(BF16)
            fresh = (fresh / total).astype(BF16).astype(F32)
            mixed = dot_nt(probs, v_buf[l, b])
            for t in range(steps):
                c = b * steps + t
                mixed = mixed + fresh[:, c:c + 1] * v_wide[c:c + 1, :]
            for t in range(steps):
                outs.append(jnp.sum(jnp.where(head_mask, mixed[16 * t:16 * t + 16, :], 0.0), axis=0, keepdims=True))
        outs.append(jnp.zeros((SLOT - seqs * steps, d), F32))
        attended = jnp.concatenate(outs, axis=0).astype(BF16)
        x = x + dot(attended, w_buf[l, :, 3 * d:4 * d]) + vec(5, l)

        hidden = layer_norm(x, vec(6, l), vec(7, l))
        h_src[l] = hidden
        broadcast(h_src.at[l], h_buf.at[l], SLOT, H0 + l)
        h_buf[l, own(h_buf, SLOT), :] = hidden
        arrived(h_buf.at[l], SLOT, H0 + l)
        act = jnp.maximum(dot(h_buf[l], f_buf[...]) + b1_pad(b1_ref, ff), 0.0)
        act = jnp.where((ff_lane >= l * ff_share) & (ff_lane < (l + 1) * ff_share), act, 0.0).astype(BF16)
        p_send[l] = dot(act, w2_ref[...])
        scatter(p_send.at[l], p_recv.at[l], SLOT, P0 + l)
        p_recv[l, own(p_recv, SLOT), :] = p_send[l, own(p_send, SLOT), :]
        arrived(p_recv.at[l], SLOT, P0 + l)
        x = x + jnp.sum(p_recv[l].reshape(n, SLOT, d), axis=0) + vec(8, l)

    final = layer_norm(x, vectors[9 * layers:9 * layers + 1, :], vectors[9 * layers + 1:9 * layers + 2, :])
    h_src[layers] = final
    broadcast(h_src.at[layers], h_buf.at[layers], SLOT, H0 + layers)
    h_buf[layers, own(h_buf, SLOT), :] = final
    arrived(h_buf.at[layers], SLOT, H0 + layers)

    def logits(c, carry):
        cols = pl.ds(pl.multiple_of(c * LANES, LANES), LANES)
        l_send[:, cols] = dot_nt(h_buf[layers], e_buf[cols, :])
        return carry

    lax.fori_loop(0, e_buf.shape[0] // LANES, logits, 0)
    scatter(l_send, lrecv, SLOT, LG)
    mine = pltpu.make_async_copy(rows(l_send, me, SLOT), rows(lrecv, me, SLOT), loc_sem.at[0])
    mine.start()

    sent(t_buf, SLOT, TP)
    sent(f_buf, share, FC)
    sent(r_buf, SLOT, EM)
    for l in range(layers):
        sent(h_buf.at[l], SLOT, H0 + l)
        sent(p_recv.at[l], SLOT, P0 + l)
        gather_sent(l)
    sent(h_buf.at[layers], SLOT, H0 + layers)
    mine.wait()
    arrived(lrecv, SLOT, LG)
    sent(lrecv, SLOT, LG)


def b1_pad(b1_ref, ff):
    return jnp.concatenate([b1_ref[...], jnp.zeros((1, ff - b1_ref.shape[1]), F32)], axis=1)


def finish_kernel(n, dims, vocab_rows, pos_ref, kv_ref, lrecv, kc_hbm, vc_hbm, logits, k_out, v_out, buf, in_sem, out_sem):
    layers, seqs, heads, steps = dims
    blocks = [(c, l, b) for l in range(layers) for b in range(seqs) for c in range(2)]
    loads = []
    for i, (c, l, b) in enumerate(blocks):
        src = (kc_hbm, vc_hbm)[c]
        loads.append(pltpu.make_async_copy(src.at[l, b], buf.at[i], in_sem.at[i]))
        loads[-1].start()
    stores = []
    per = n // len(blocks) + 1
    for i, (c, l, b) in enumerate(blocks):
        for j in range(i * per, min(n, (i + 1) * per)):
            part = lrecv[SLOT * j:SLOT * j + SLOT, 0:vocab_rows]
            for s in range(seqs):
                logits[s, :, vocab_rows * j:vocab_rows * (j + 1)] = part[s * steps:(s + 1) * steps, :]
        loads[i].wait()
        for t in range(steps):
            p = pos_ref[b] + t
            tile = pl.ds(pl.multiple_of(p // LANES * LANES, LANES), LANES)
            row = b * steps + t
            fresh = jnp.broadcast_to(kv_ref[l, c, :, row:row + 1], (buf.shape[1], LANES))
            hit = iota((buf.shape[1], LANES), 1) == lax.rem(p, LANES)
            old = buf[i, :, tile].astype(F32)
            buf[i, :, tile] = jnp.where(hit, fresh, old).astype(BF16)
        dst = (k_out, v_out)[c]
        stores.append(pltpu.make_async_copy(buf.at[i], dst.at[l, b], out_sem.at[i]))
        stores[-1].start()
    for copy in stores:
        copy.wait()


def solution(mesh):
    batch_axes = ("rep", "dp")
    mat_spec = P(None, "dp", None)
    vec_spec = P(None, "dp")
    in_specs = (P(None, batch_axes), P(batch_axes), P(None, batch_axes), P(None, batch_axes), P("dp", None), P("dp", None), vec_spec, vec_spec, mat_spec, mat_spec, mat_spec, vec_spec, vec_spec, vec_spec, mat_spec, vec_spec, vec_spec, vec_spec, mat_spec, vec_spec, mat_spec, vec_spec, P("dp"), P("dp"))
    out_specs = (P(None, batch_axes, None), P(None, batch_axes), P(None, batch_axes))
    n = mesh.shape["dp"]

    def body(tokens, start_pos, k_cache, v_cache, tok_table, pos_table, ln1_gain, ln1_bias, w_q, w_k, w_v, b_q, b_k, b_v, w_o, b_o, ln2_gain, ln2_bias, w_fc1, b_fc1, w_fc2, b_fc2, lnf_gain, lnf_bias):
        layers, seqs, heads, length, head_dim = k_cache.shape
        steps = tokens.shape[0]
        d = heads * head_dim
        share = w_q.shape[1]
        vocab_rows = tok_table.shape[0]
        main = vocab_rows // LANES * LANES
        count = seqs * steps
        ff_share = b_fc1.shape[1]
        ff = -(-(layers * ff_share + 32) // LANES) * LANES

        tok = jnp.pad(tokens.T.reshape(count, 1), ((0, SLOT - count), (0, 0)), constant_values=-1)
        place = (start_pos[:, None] + jnp.arange(steps, dtype=jnp.int32)[None, :]).reshape(count, 1)
        place = jnp.pad(place, ((0, SLOT - count), (0, 0)), constant_values=-1)
        tp = jnp.where(jnp.arange(LANES)[None, :] < LANES // 2, tok, place)
        wa = jnp.concatenate([w_q, w_k, w_v, w_o], axis=-1)
        vecs = jnp.concatenate([ln1_gain, ln1_bias, b_q, b_k, b_v, b_o, ln2_gain, ln2_bias, b_fc2,
                                lnf_gain[None], lnf_bias[None]], axis=0)
        fs = w_fc1.reshape(layers, share, n, ff_share).transpose(2, 1, 0, 3).reshape(n, share, layers * ff_share)
        vecs = jnp.broadcast_to(vecs.T[None], (n, share, vecs.shape[0]))
        fs = jnp.concatenate([fs, vecs], axis=-1)
        fs = jnp.pad(fs, ((0, 0), (0, 0), (0, ff - fs.shape[-1]))).reshape(n * share, ff)
        w2 = jnp.pad(w_fc2.reshape(layers * ff_share, d), ((0, ff - layers * ff_share), (0, 0)))
        b1 = b_fc1.astype(F32).reshape(1, layers * ff_share)
        tail = jnp.pad(tok_table[main:], ((0, main + LANES - vocab_rows), (0, 0)))
        kc = jnp.swapaxes(k_cache, 3, 4).reshape(layers, seqs, d, length)
        vc = jnp.swapaxes(v_cache, 3, 4).reshape(layers, seqs, d, length)

        dims = (layers, seqs, heads, steps)
        vmem = pl.BlockSpec(memory_space=pltpu.VMEM)
        anym = pl.BlockSpec(memory_space=pl.ANY)
        smem = pl.BlockSpec(memory_space=pltpu.SMEM)
        side = math.isqrt(n // 2)
        phases = 4 + 2 * layers + 1
        lrecv, kv_new = pl.pallas_call(
            functools.partial(decode_kernel, n, dims),
            out_shape=(jax.ShapeDtypeStruct((n * SLOT, main + LANES), F32),
                       jax.ShapeDtypeStruct((layers, 2, SLOT, d), BF16)),
            in_specs=[smem, vmem, anym, vmem, vmem, vmem, vmem, vmem, vmem, anym, anym],
            out_specs=(anym, vmem),
            scratch_shapes=[
                pltpu.VMEM((n * SLOT, LANES), jnp.int32),
                pltpu.VMEM((main + LANES, d), BF16),
                pltpu.VMEM((n * SLOT, 2 * d), BF16),
                pltpu.VMEM((n * SLOT, 2 * d), BF16),
                pltpu.VMEM((layers, n * share, 4 * d), BF16),
                pltpu.VMEM((n * share, ff), BF16),
                pltpu.VMEM((layers, seqs, d, length), BF16),
                pltpu.VMEM((layers, seqs, d, length), BF16),
                pltpu.VMEM((layers + 1, SLOT, d), BF16),
                pltpu.VMEM((layers + 1, n * SLOT, d), BF16),
                pltpu.VMEM((layers, n * SLOT, d), F32),
                pltpu.VMEM((layers, n * SLOT, d), F32),
                pltpu.VMEM((n * SLOT, main + LANES), F32),
                pltpu.SemaphoreType.DMA((1 + 2 * layers,)),
                pltpu.SemaphoreType.DMA((phases,)),
                pltpu.SemaphoreType.DMA((phases,)),
                pltpu.SemaphoreType.DMA((layers, 2)),
                pltpu.SemaphoreType.DMA((layers, 2, side - 1)),
                pltpu.SemaphoreType.DMA((layers, 2, side, side - 1)),
                pltpu.SemaphoreType.DMA((layers,)),
            ],
            compiler_params=pltpu.CompilerParams(collective_id=0, has_side_effects=True, vmem_limit_bytes=62 * 2 ** 20),
            name="decode",
        )(start_pos, tp, tok_table, tail, pos_table, wa, fs, w2, b1, kc, vc)

        kv_t = jnp.swapaxes(kv_new, 2, 3).astype(F32)
        logits, k_out, v_out = pl.pallas_call(
            functools.partial(finish_kernel, n, dims, vocab_rows),
            out_shape=(jax.ShapeDtypeStruct((seqs, steps, n * vocab_rows), F32),
                       jax.ShapeDtypeStruct(kc.shape, BF16), jax.ShapeDtypeStruct(vc.shape, BF16)),
            in_specs=[smem, vmem, vmem, anym, anym],
            out_specs=(vmem, anym, anym),
            scratch_shapes=[
                pltpu.VMEM((2 * layers * seqs, d, length), BF16),
                pltpu.SemaphoreType.DMA((2 * layers * seqs,)),
                pltpu.SemaphoreType.DMA((2 * layers * seqs,)),
            ],
            compiler_params=pltpu.CompilerParams(vmem_limit_bytes=60 * 2 ** 20),
            name="finish",
        )(start_pos, kv_t, lrecv, kc, vc)

        def unfold(cache):
            return jnp.swapaxes(cache.reshape(layers, seqs, heads, head_dim, length), 3, 4)

        return jnp.swapaxes(logits, 0, 1), unfold(k_out), unfold(v_out)

    return jax.shard_map(body, mesh=mesh, in_specs=in_specs, out_specs=out_specs, check_vma=False)
```

time: 876 us -> 185 us (0.21)
  waiting for transfers between devices: 536 us -> 0 us
  Pallas kernels: 0 us -> 167 us
  matrix products: 130 us -> 0 us
  local copies, waits for them, and re-layouts: 100 us -> 12 us
  blocking collectives: 51.8 us -> 0 us
  other arithmetic: 33.7 us -> 4.04 us
  between operations: 15.3 us -> 0.68 us
    all_gather x14 -> x0, waiting for transfers between devices: 531 us -> none  [gather(): return lax.all_gather(piece, 'dp', axis=0, tiled=True)]
    pallas_call x0 -> x2, Pallas kernels: none -> 167 us  [the longest x1 151 us: body(): pl.pallas_call(functools.partial(decode_kernel, n, dims), out_shape=(jax....]
    dot_general x30 -> x0, matrix products: 130 us -> none  [the longest x2 58.9 us: body(): jnp.einsum('bd,vd->bv', final, table, preferred_element_type=jnp.float32)]
    unnamed x90 -> x0, local copies, waits for them, and re-layouts: 81.1 us -> none
    unnamed x1 -> x0, blocking collectives: 51.8 us -> none
    another operation x3 -> x0, other arithmetic: 17.1 us -> none  [body(): return (jnp.stack(outputs), jnp.stack(k_layers), jnp.stack(v_layers))]
    select_n x2 -> x1, other arithmetic: 13.2 us -> 0.67 us  [body(): tp = jnp.where(jnp.arange(LANES)[None, :] < LANES // 2, tok, place)]
  transfers between devices with their start and end apart: 14 -> 0, of which waited for: 11 -> 0; matrix products, arithmetic and copies ran while one was open for 19% -> 0% of each run, Pallas kernels for 0% -> 0%
where the time goes in v1:
time: 185 us; the launch traced here: 184 us
  Pallas kernels  167 us (90%)
  local copies, waits for them, and re-layouts  12 us (6%)
  other arithmetic  4.04 us (2%)
    pallas_call x1, Pallas kernels, body(): pl.pallas_call(functools.partial(decode_kernel, n, dims), out_shape=(jax....  151 us
    pallas_call x1, Pallas kernels, body(): pl.pallas_call(functools.partial(finish_kernel, n, dims, vocab_rows), out...  16.4 us

profile of v1, /device:TPU:97, one launch (start us, length us, event | category | flops | bytes accessed | tf_op | source)
XLA Modules:
  0.0 184.2 jit_solution(1277875084942557620)
XLA Ops:
  0.6 1.3 reshape.80.b1_ref
  2.0 0.8 copy.31
  2.7 0.1 reshape.68
  2.8 0.7 iota_add_fusion
  3.5 0.1 add.36
  3.6 0.7 broadcast_select_fusion.tp_ref
  4.3 2.2 %concatenate.10 = bf16[20,24]{1,0:T(8,128)(2,1)S(1)} concatenate(bf16[2,24]{1,0:T(2,128)(2,1)} %param.30, bf16[2,24]{1,0:T(2,128)(2,1)} %param.31, bf16[2,24]{1,0:T(2,128)(2,1)} %param.35, bf16[2,24]{1,0:T(2,128)(2,1)} %param.36, bf16[2,24]{1,0:T(2,128)(2,1)} %param.37, bf16[2,24]{1,0:T(2,128)(2,1)} %param.39, bf16[2,24]{1,0:T(2,128)(2,1)} %param.40, bf16[2,24]{1,0:T(2,128)(2,1)} %param.41, ...), dimensions={0} | concatenate | bytes 1920 | tf_op jit(solution)/shard_map/concatenate | solution.py:352
  6.5 0.1 copy.33
  6.6 0.8 slice.3
  7.4 0.7 pad.21.tok_tail
  8.1 1.7 pad_maximum_fusion.wa_ref
  9.8 1.4 reshape.69
  11.2 0.4 copy.32
  11.6 0.2 reshape.70
  11.8 0.9 fusion.2
  12.7 1.7 pad.23.w2_ref
  14.5 151.0 %decode.1 = (f32[256,1664]{1,0:T(8,128)}, bf16[2,2,8,768]{3,2,1,0:T(8,128)(2,1)}) custom-call(s32[3]{0:T(128)} %pos_ref.3, s32[8,128]{1,0:T(8,128)} %broadcast_select_fusion.tp_ref, bf16[1571,768]{1,0:T(8,128)(2,1)} %tok_hbm.1, bf16[128,768]{1,0:T(8,128)(2,1)} %pad.21.tok_tail, bf16[64,768]{1,0:T(8,128)(2,1)} %pos_tab.1, ...), custom_call_target="tpu_custom_call" | custom-call | tf_op jit(solution)/shard_map/decode/pallas_call | solution.py:370
  165.5 2.2 %copy.34 = f32[2,2,8,768]{2,3,1,0:T(8,128)} copy(bf16[2,2,8,768]{3,2,1,0:T(8,128)(2,1)} %get-tuple-element.8) | data formatting | bytes 147456 | tf_op jit(solution)/shard_map/convert_element_type | solution.py:402
  167.7 16.4 %finish.1 = (f32[3,2,50272]{2,1,0:T(2,128)}, bf16[2,3,768,1024]{3,2,1,0:T(8,128)(2,1)}, bf16[2,3,768,1024]{3,2,1,0:T(8,128)(2,1)}) custom-call(s32[3]{0:T(128)} %pos_ref.3, f32[2,2,768,8]{3,2,1,0:T(8,128)} %bitcast.29, f32[256,1664]{1,0:T(8,128)} %get-tuple-element.9.lrecv, bf16[2,3,768,1024]{3,2,1,0:T(8,128)(2,1)} %bitcast.26, ...), custom_call_target="tpu_custom_call" | custom-call | tf_op jit(solution)/shard_map/finish/pallas_call | solution.py:403
  (3 shorter events, 0.0 us)
